TPU v7x, 32 devices: a whole 2x2x4 slice. The times are simulated.
32 devices in a mesh: section: 4 (over y, x), dp: 8 (over z, core).
Axes of the slice: x: 2, y: 2, z: 4, core: 2. Of those that a mesh axis runs over, the one named last changes fastest.
Arguments:
- block_inputs: bfloat16 [4, 4, 512, 2048], P('section', None, 'dp'), may hold values from -6 to 6
- mixed_inputs: bfloat16 [4, 4, 512, 2048], P('section', None, 'dp'), may hold values from -6 to 6
- token_ids: int32 [4, 512], P(None, 'dp'), may hold values from 0 to 2047
- target_ids: int32 [4, 512], P(None, 'dp'), may hold values from 0 to 2047
- final_gain: float32 [2048], replicated, may hold values from 0.5 to 1.5
- out_weight: bfloat16 [4, 2048, 2048], P('section'), may hold values from -0.0625 to 0.0625
- head_weight: bfloat16 [2048, 2048], P('section'), may hold values from -0.375 to 0.375
- out_master: float32 [4, 2048, 2048], P('section', 'dp'), may hold values from -0.125 to 0.125
- out_first: float32 [4, 2048, 2048], P('section', 'dp'), may hold values from -1.25 to 1.25
- out_second: float32 [4, 2048, 2048], P('section', 'dp'), may hold values from 1 to 20
- head_master: float32 [2048, 2048], P(('section', 'dp')), may hold values from -0.125 to 0.125
- head_first: float32 [2048, 2048], P(('section', 'dp')), may hold values from -0.75 to 0.75
- head_second: float32 [2048, 2048], P(('section', 'dp')), may hold values from 0.3 to 6
- embed_master: float32 [2048, 2048], P(('section', 'dp')), may hold values from -0.125 to 0.125
- embed_first: float32 [2048, 2048], P(('section', 'dp')), may hold values from -0.0625 to 0.0625
- embed_second: float32 [2048, 2048], P(('section', 'dp')), may hold values from 0.0024414062 to 0.048828125
Outputs:
- out_master_next: float32 [4, 2048, 2048], P('section', 'dp')
- out_first_next: float32 [4, 2048, 2048], P('section', 'dp')
- out_second_next: float32 [4, 2048, 2048], P('section', 'dp')
- head_master_next: float32 [2048, 2048], P(('section', 'dp'))
- head_first_next: float32 [2048, 2048], P(('section', 'dp'))
- head_second_next: float32 [2048, 2048], P(('section', 'dp'))
- embed_master_next: float32 [2048, 2048], P(('section', 'dp'))
- embed_first_next: float32 [2048, 2048], P(('section', 'dp'))
- embed_second_next: float32 [2048, 2048], P(('section', 'dp'))
Inputs may be any that keep to these rules, and one draw needn't show every extreme that they name: `token_ids`: every token id lies in 0 to 2047. `target_ids`: every target id lies in 0 to 2047.
All inputs are finite; a program needn't handle non-finite values.
Results may differ from a plain program's by a relative error of at most 0.00155.
Values may be sent and summed in bfloat16 or wider, within the bound.
A program may use at most 128 MiB of HBM per device.

v0:
```python
import jax
import jax.numpy as jnp
from jax import lax
from jax.sharding import PartitionSpec as P

norm_eps = 1e-05
beta_first = 0.9
beta_second = 0.95
adam_eps = 1e-05
learning_rate = 0.0003
decay_rate = 0.1


def broadcast(value, axis, source):
    kept = jnp.where(lax.axis_index(axis) == source, value, 0).astype(value.dtype)
    return lax.psum(kept, axis)


def combined_all(part, axis, combine):
    gathered = jax.tree.map(lambda a: lax.all_gather(a, axis), part)

    def take(source):
        return jax.tree.map(lambda a: lax.dynamic_index_in_dim(a, source, 0, False), gathered)

    return lax.fori_loop(
        1, lax.axis_size(axis), lambda source, state: combine(state, take(source)), take(0)
    )


def from_behind(block, axis, distance):
    devices = range(lax.axis_size(axis))
    route = [(i - distance, i) for i in devices if i - distance in devices]
    return lax.ppermute(block, axis, route)


def times_transposed(former, latter):
    return lax.dot_general(
        former, latter, (((1,), (1,)), ((), ())), preferred_element_type=jnp.float32
    )


def transposed_times(former, latter):
    return lax.dot_general(
        former, latter, (((0,), (0,)), ((), ())), preferred_element_type=jnp.float32
    )


def plain_times(former, latter):
    return jnp.dot(former, latter, preferred_element_type=jnp.float32)


def normalize(values, gain):
    inverse = lax.rsqrt(jnp.mean(values * values, axis=-1, keepdims=True) + norm_eps)
    return (inverse, values * inverse * gain)


def norm_backward(values, inverse, scaled_cotangent):
    unit = values * inverse
    return inverse * (
        scaled_cotangent - unit * jnp.mean(scaled_cotangent * unit, axis=-1, keepdims=True)
    )


def adam_update(master, first, second, gradient):
    first_next = beta_first * first + (1.0 - beta_first) * gradient
    second_next = beta_second * second + (1.0 - beta_second) * gradient * gradient
    master_next = master - learning_rate * (
        first_next / (jnp.sqrt(second_next) + adam_eps) + decay_rate * master
    )
    return (master_next, first_next, second_next)


def join_rows(former, latter):
    top = jnp.maximum(former[0], latter[0])
    return (top, former[1] * jnp.exp(former[0] - top) + latter[1] * jnp.exp(latter[0] - top))


def local(
    block_inputs,
    mixed_inputs,
    token_ids,
    target_ids,
    final_gain,
    out_weight,
    head_weight,
    out_master,
    out_first,
    out_second,
    head_master,
    head_first,
    head_second,
    embed_master,
    embed_first,
    embed_second,
):
    sections = lax.axis_size("section")
    section = lax.axis_index("section")
    last = sections - 1
    batches, rows, width = mixed_inputs[0].shape
    flat_mixed = mixed_inputs[0].reshape(batches * rows, width)
    wide = block_inputs[0].reshape(batches * rows, width).astype(jnp.float32)
    slice_rows = head_weight.shape[0]
    vocabulary_start = section * slice_rows
    columns = vocabulary_start + lax.broadcasted_iota(jnp.int32, (1, slice_rows), 1)
    final = wide + times_transposed(flat_mixed, out_weight[0])
    final_inverse, final_scaled = normalize(final, final_gain)
    shared_hidden = broadcast(final_scaled.astype(jnp.bfloat16), "section", last)
    logits = times_transposed(shared_hidden, head_weight)
    local_top = jnp.max(logits, axis=1)
    local_weights = jnp.exp(logits - local_top[:, None])
    row_top, row_total = combined_all(
        (local_top, jnp.sum(local_weights, axis=1)), "section", join_rows
    )
    predicted = local_weights * (jnp.exp(local_top - row_top) / row_total)[:, None]
    target_flat = target_ids.reshape(-1)
    logit_cotangent = jnp.where(target_flat[:, None] == columns, predicted - 1.0, predicted).astype(
        jnp.bfloat16
    )
    hidden_cotangent = lax.psum(plain_times(logit_cotangent, head_weight), "section")
    top_cotangent = norm_backward(final, final_inverse, hidden_cotangent * final_gain).astype(
        jnp.bfloat16
    )

    def reduce_head():

        def head_term(count):
            part = lax.slice_in_dim(logit_cotangent, 0, count, axis=1)
            return transposed_times(part, shared_hidden)

        return lax.psum_scatter(
            head_term(head_master.shape[0] * lax.axis_size("dp")),
            "dp",
            scatter_dimension=0,
            tiled=True,
        )

    def relay(step, held):
        received = from_behind(held, "section", -1)
        return jnp.where(section == last, held, received)

    cotangent = lax.fori_loop(0, last, relay, top_cotangent)
    out_term = transposed_times(cotangent, flat_mixed)
    out_gradient = lax.psum_scatter(out_term, "dp", scatter_dimension=0, tiled=True)
    tokens_flat = token_ids.reshape(-1)

    def embed_term(count):
        wanted = vocabulary_start + lax.broadcasted_iota(jnp.int32, (1, count), 1)
        marks = (tokens_flat[:, None] == wanted).astype(jnp.bfloat16)
        return transposed_times(marks, cotangent)

    embed_gradient = lax.psum_scatter(
        embed_term(embed_master.shape[0] * lax.axis_size("dp")),
        "dp",
        scatter_dimension=0,
        tiled=True,
    )
    head_gradient = reduce_head()
    out_out = adam_update(out_master, out_first, out_second, out_gradient.reshape(out_master.shape))
    head_out = adam_update(head_master, head_first, head_second, head_gradient)
    embed_out = adam_update(embed_master, embed_first, embed_second, embed_gradient)
    return (
        out_out[0],
        out_out[1],
        out_out[2],
        head_out[0],
        head_out[1],
        head_out[2],
        embed_out[0],
        embed_out[1],
        embed_out[2],
    )


def solution(mesh):
    return jax.shard_map(
        local,
        mesh=mesh,
        in_specs=(
            P("section", None, "dp", None),
            P("section", None, "dp", None),
            P(None, "dp"),
            P(None, "dp"),
            P(),
            P("section", None, None),
            P("section", None),
            P("section", "dp", None),
            P("section", "dp", None),
            P("section", "dp", None),
            P(("section", "dp"), None),
            P(("section", "dp"), None),
            P(("section", "dp"), None),
            P(("section", "dp"), None),
            P(("section", "dp"), None),
            P(("section", "dp"), None),
        ),
        out_specs=(
            P("section", "dp", None),
            P("section", "dp", None),
            P("section", "dp", None),
            P(("section", "dp"), None),
            P(("section", "dp"), None),
            P(("section", "dp"), None),
            P(("section", "dp"), None),
            P(("section", "dp"), None),
            P(("section", "dp"), None),
        ),
        check_vma=False,
    )
```

profile of v0, /device:TPU:0, one launch (start us, length us, event | category | flops | bytes accessed | tf_op | source)
XLA Modules:
  0.0 482.8 jit_solution(1719331455801563350)
XLA Ops:
  7.3 7.8 %multiply_reduce_fusion.1 = (f32[256]{0:T(256)S(1)}, f32[256,2048]{1,0:T(8,128)}) fusion(bf16[256,2048]{1,0:T(8,128)(2,1)} %bitcast.42, bf16[1,2048,2048]{2,1,0:T(8,128)(2,1)} %param.25, bf16[256,2048]{1,0:T(8,128)(2,1)} %bitcast.52), kind=kOutput, calls=%fused_computation.15 | convolution fusion | flops 2149580544 | bytes 12583936 | tf_op jit(solution)/shard_map/dot_general | solution.py:37
  15.1 2.9 fusion.7
  18.1 55.2 %all-reduce.3.cloned.1.call-done = bf16[256,2048]{1,0:T(8,128)(2,1)} async-done(((bf16[256,2048]{1,0:T(8,128)(2,1)}), bf16[256,2048]{1,0:T(8,128)(2,1)}) %all-reduce.3.cloned.1.call-update) | async-done | bytes 1048592 | tf_op jit(solution)/shard_map/psum | solution.py:16
  73.3 2.0 fusion.23
  75.6 8.0 %all-gather.3 = f32[4,1,256]{2,1,0:T(1,128)S(1)} all-gather(f32[1,1,256]{2,1,0:T(1,128)S(1)} %bitcast.51), channel_id=3, replica_groups=mesh['section'=4,'dp'=8] {'section'}, dimensions={0}, use_global_device_ids=true | all-gather | bytes 5120 | tf_op jit(solution)/shard_map/all_gather | solution.py:20
  83.6 7.1 %all-gather.2 = f32[4,1,256]{2,1,0:T(1,128)S(1)} all-gather(f32[1,1,256]{2,1,0:T(1,128)S(1)} %bitcast.46), channel_id=2, replica_groups=mesh['section'=4,'dp'=8] {'section'}, dimensions={0}, use_global_device_ids=true | all-gather | bytes 5120 | tf_op jit(solution)/shard_map/all_gather | solution.py:20
  90.9 2.1 fusion.18
  93.1 1.1 copy-done.6
  94.3 2.9 fusion.16
  97.2 0.6 copy-done.15
  97.9 64.8 %all-reduce.5.cloned.1.call-done = f32[256,2048]{1,0:T(8,128)} async-done(((f32[256,2048]{1,0:T(8,128)}), f32[256,2048]{1,0:T(8,128)}) %all-reduce.5.cloned.1.call-update) | async-done | bytes 2097168 | tf_op jit(solution)/shard_map/psum | solution.py:119
  162.7 2.1 multiply_reduce_fusion
  164.9 0.6 copy-done.4
  165.6 0.5 multiply_convert_fusion
  166.0 79.9 %while.30 = (s32[]{:T(128)}, bf16[256,2048]{1,0:T(8,128)(2,1)S(1)}, pred[]{:T(512)}, s32[]{:T(128)}) while((s32[]{:T(128)}, bf16[256,2048]{1,0:T(8,128)(2,1)S(1)}, pred[]{:T(512)}, s32[]{:T(128)}) %tuple.77), condition=%wide.region_9.10_spmd, body=%wide.region_8.9_spmd.sunk | while | flops 524290 | bytes 7340126 | solution.py:141
  166.1 1.3 collective-permute-start
  167.4 25.3 %collective-permute-done = bf16[256,2048]{1,0:T(8,128)(2,1)S(1)} collective-permute-done((bf16[256,2048]{1,0:T(8,128)(2,1)S(1)}, bf16[256,2048]{1,0:T(8,128)(2,1)S(1)}, u32[]{:S(2)}, u32[]{:S(2)}) %collective-permute-start) | collective-permute-done | bytes 1048608 | tf_op jit(solution)/shard_map/while/body/eval_jaxpr/ppermute | solution.py:33
  193.0 1.3 collective-permute-start
  194.3 25.2 %collective-permute-done = bf16[256,2048]{1,0:T(8,128)(2,1)S(1)} collective-permute-done((bf16[256,2048]{1,0:T(8,128)(2,1)S(1)}, bf16[256,2048]{1,0:T(8,128)(2,1)S(1)}, u32[]{:S(2)}, u32[]{:S(2)}) %collective-permute-start) | collective-permute-done | bytes 1048608 | tf_op jit(solution)/shard_map/while/body/eval_jaxpr/ppermute | solution.py:33
  219.5 0.3 broadcast_select_fusion.2
  219.8 1.3 collective-permute-start
  221.1 24.6 %collective-permute-done = bf16[256,2048]{1,0:T(8,128)(2,1)S(1)} collective-permute-done((bf16[256,2048]{1,0:T(8,128)(2,1)S(1)}, bf16[256,2048]{1,0:T(8,128)(2,1)S(1)}, u32[]{:S(2)}, u32[]{:S(2)}) %collective-permute-start) | collective-permute-done | bytes 1048608 | tf_op jit(solution)/shard_map/while/body/eval_jaxpr/ppermute | solution.py:33
  245.7 0.3 broadcast_select_fusion.2
  246.0 2.8 fusion.11
  249.0 1.0 copy-done.5
  250.0 8.3 %fusion.24 = f32[2048,2048]{1,0:T(8,128)} fusion(bf16[256,2048]{1,0:T(8,128)(2,1)S(1)} %get-tuple-element.183, bf16[256,2048]{1,0:T(8,128)(2,1)S(1)} %bitcast.43), kind=kOutput, calls=%fused_computation.42 | convolution fusion | flops 2147483648 | bytes 18874368 | tf_op jit(solution)/shard_map/dot_general | solution.py:43
  258.4 0.9 copy-done.7
  259.7 2.4 multiply_subtract_fusion.2
  262.1 37.8 %reduce-scatter.8.cloned.1.call-done = f32[64,2048]{1,0:T(8,128)} async-done(((f32[512,2048]{1,0:T(8,128)}), f32[64,2048]{1,0:T(8,128)}) %reduce-scatter.8.cloned.1.call-update) | async-done | bytes 524304 | tf_op jit(solution)/shard_map/reduce_scatter | solution.py:151
  299.9 2.4 multiply_subtract_fusion.1
  302.2 166.4 %reduce-scatter.4.cloned.1.call-done = f32[256,2048]{1,0:T(8,128)} async-done(((f32[2048,2048]{1,0:T(8,128)}), f32[256,2048]{1,0:T(8,128)}) %reduce-scatter.4.cloned.1.call-update) | async-done | bytes 2097168 | tf_op jit(solution)/shard_map/reduce_scatter | solution.py:143
  468.7 7.6 %multiply_subtract_fusion = (f32[1,256,2048]{2,1,0:T(8,128)}, f32[1,256,2048]{2,1,0:T(8,128)}, f32[1,256,2048]{2,1,0:T(8,128)}) fusion(f32[1,256,2048]{2,1,0:T(8,128)} %param.27, f32[256,2048]{1,0:T(8,128)} %reduce-scatter.4.cloned.1.call-done, f32[1,256,2048]{2,1,0:T(8,128)} %param.29, f32[1,256,2048]{2,1,0:T(8,128)} %param.28), kind=kLoop, calls=%fused_computation.11 | loop fusion | flops 6815744 | bytes 14680064 | tf_op jit(solution)/shard_map/sub | solution.py:67
  (57 shorter events, 1.9 us)
Async XLA Ops:
  7.2 66.1 %copy-start = (bf16[512,2048]{1,0:T(8,128)(2,1)S(1)}, bf16[512,2048]{1,0:T(8,128)(2,1)}, u32[]{:S(2)}) copy-start(bf16[512,2048]{1,0:T(8,128)(2,1)} %param.26) | copy-start | bytes 6291460
  7.2 66.1 %all-reduce.3.cloned.1.call-start = ((), (), s32[]{:S(2)}) async-start(), calls=%async_computation.3 | async-start | bytes 2097152 | tf_op jit(solution)/shard_map/psum | solution.py:16
  7.2 7.8 %copy-start.13 = (f32[2048]{0:T(1024)S(1)}, f32[2048]{0:T(1024)}, u32[]{:S(2)}) copy-start(f32[2048]{0:T(1024)} %param.24) | copy-start | bytes 24580
  15.1 3.0 copy-start.14
  18.0 144.7 %all-reduce.5.cloned.1.call-start = ((), (), s32[]{:S(2)}) async-start(), calls=%async_computation.4 | async-start | bytes 4194304 | tf_op jit(solution)/shard_map/psum | solution.py:119
  93.0 1.2 copy-start.6
  93.1 165.4 %reduce-scatter.6.cloned.1.call-start = ((), (), s32[]{:S(2)}) async-start(), calls=%async_computation.6 | async-start | bytes 4718592 | tf_op jit(solution)/shard_map/reduce_scatter | solution.py:130
  97.1 0.7 copy-start.15
  97.1 65.6 %copy-start.2 = (f32[256,2048]{1,0:T(8,128)S(1)}, f32[256,2048]{1,0:T(8,128)}, u32[]{:S(2)}) copy-start(f32[256,2048]{1,0:T(8,128)} %get-tuple-element.214) | copy-start | bytes 6291460
  97.1 202.7 %reduce-scatter.8.cloned.1.call-start = ((), (), s32[]{:S(2)}) async-start(), calls=%async_computation.7 | async-start | bytes 4718592 | tf_op jit(solution)/shard_map/reduce_scatter | solution.py:151
  162.7 2.2 copy-start.3
  162.7 2.9 copy-start.4
  166.1 26.6 %collective-permute-start = (bf16[256,2048]{1,0:T(8,128)(2,1)S(1)}, bf16[256,2048]{1,0:T(8,128)(2,1)S(1)}, u32[]{:S(2)}, u32[]{:S(2)}) collective-permute-start(bf16[256,2048]{1,0:T(8,128)(2,1)S(1)} %get-tuple-element.304), channel_id=1, source_target_pairs={{8,0},{16,8},{24,16},{9,1},{17,9},{25,17},{10,2},{18,10},{26,18},{... | collective-permute-start | bytes 3145736 | tf_op jit(solution)/shard_map/while/body/eval_jaxpr/ppermute | solution.py:33
  193.0 26.5 %collective-permute-start = (bf16[256,2048]{1,0:T(8,128)(2,1)S(1)}, bf16[256,2048]{1,0:T(8,128)(2,1)S(1)}, u32[]{:S(2)}, u32[]{:S(2)}) collective-permute-start(bf16[256,2048]{1,0:T(8,128)(2,1)S(1)} %get-tuple-element.304), channel_id=1, source_target_pairs={{8,0},{16,8},{24,16},{9,1},{17,9},{25,17},{10,2},{18,10},{26,18},{... | collective-permute-start | bytes 3145736 | tf_op jit(solution)/shard_map/while/body/eval_jaxpr/ppermute | solution.py:33
  219.8 25.9 %collective-permute-start = (bf16[256,2048]{1,0:T(8,128)(2,1)S(1)}, bf16[256,2048]{1,0:T(8,128)(2,1)S(1)}, u32[]{:S(2)}, u32[]{:S(2)}) collective-permute-start(bf16[256,2048]{1,0:T(8,128)(2,1)S(1)} %get-tuple-element.304), channel_id=1, source_target_pairs={{8,0},{16,8},{24,16},{9,1},{17,9},{25,17},{10,2},{18,10},{26,18},{... | collective-permute-start | bytes 3145736 | tf_op jit(solution)/shard_map/while/body/eval_jaxpr/ppermute | solution.py:33
  248.8 1.2 copy-start.5
  248.8 219.9 %reduce-scatter.4.cloned.1.call-start = ((), (), s32[]{:S(2)}) async-start(), calls=%async_computation.5 | async-start | bytes 18874368 | tf_op jit(solution)/shard_map/reduce_scatter | solution.py:143
  258.3 1.0 copy-start.7
  258.3 1.2 copy-start.8
  258.3 1.4 copy-start.9
  258.4 41.5 %copy-start.10 = (f32[64,2048]{1,0:T(8,128)S(1)}, f32[64,2048]{1,0:T(8,128)}, u32[]{:S(2)}) copy-start(f32[64,2048]{1,0:T(8,128)} %param.33) | copy-start | bytes 1572868
  258.4 41.5 %copy-start.11 = (f32[64,2048]{1,0:T(8,128)S(1)}, f32[64,2048]{1,0:T(8,128)}, u32[]{:S(2)}) copy-start(f32[64,2048]{1,0:T(8,128)} %param.35) | copy-start | bytes 1572868
  258.4 41.5 %copy-start.12 = (f32[64,2048]{1,0:T(8,128)S(1)}, f32[64,2048]{1,0:T(8,128)}, u32[]{:S(2)}) copy-start(f32[64,2048]{1,0:T(8,128)} %param.34) | copy-start | bytes 1572868
  468.7 7.6 %copy-start.1 = (bf16[512,2048]{1,0:T(8,128)(2,1)S(1)}, bf16[512,2048]{1,0:T(8,128)(2,1)}, u32[]{:S(2)}) copy-start(bf16[512,2048]{1,0:T(8,128)(2,1)} %param.26) | copy-start | bytes 6291460
Sparse Core Ops, SparseCore 0:
  18.1 55.1 all-reduce.2
  93.2 69.4 all-reduce.4
  165.0 49.8 reduce-scatter.5
  248.9 50.8 reduce-scatter.7
  302.0 166.5 reduce-scatter.3
where the time goes:
time: 483 us
  waiting for transfers between devices  399 us (83%)
  matrix products  26 us (5%)
  other arithmetic  19 us (4%)
  blocking collectives  15.2 us (3%)
  between operations  13.9 us (3%)
  local copies, waits for them, and re-layouts  4.92 us (1%)
    reduce_scatter x1, waiting for transfers between devices, local(): lax.psum_scatter(out_term, 'dp', scatter_dimension=0, tiled=True)  166 us
    ppermute x3, waiting for transfers between devices, from_behind(): return lax.ppermute(block, axis, route)  75.1 us
    psum x1, waiting for transfers between devices, local(): lax.psum(plain_times(logit_cotangent, head_weight), 'section')  64.8 us
    psum x1, waiting for transfers between devices, broadcast(): return lax.psum(kept, axis)  55.2 us
    reduce_scatter x1, waiting for transfers between devices, local(): lax.psum_scatter(embed_term(embed_master.shape[0] * lax.axis_size('dp')),...  37.8 us
    all_gather x2, blocking collectives, combined_all(): gathered = jax.tree.map(lambda a: lax.all_gather(a, axis), part)  15.2 us
    dot_general x3, matrix products, transposed_times(): lax.dot_general(former, latter, (((0,), (0,)), ((), ())), preferred_eleme...  14 us
    sub x3, other arithmetic, adam_update(): master - learning_rate * (first_next / (jnp.sqrt(second_next) + adam_eps)...  12.3 us
  transfers between devices with their start and end apart: 8, of which 7 were waited for; matrix products, arithmetic and copies ran while one was open for 5% of the time, Pallas kernels for 0%

commit v1 on v0

--- a/solution.py
+++ b/solution.py
@@ -9,6 +9,11 @@
 adam_eps = 1e-05
 learning_rate = 0.0003
 decay_rate = 0.1
+
+
+def _save_bars(mine, a_name):
+    tmp = jnp.sum(lax.all_gather(mine, axis_name=a_name), axis=0)
+    return tmp
 
 
 def broadcast(value, axis, source):
@@ -116,7 +121,7 @@
     logit_cotangent = jnp.where(target_flat[:, None] == columns, predicted - 1.0, predicted).astype(
         jnp.bfloat16
     )
-    hidden_cotangent = lax.psum(plain_times(logit_cotangent, head_weight), "section")
+    hidden_cotangent = _save_bars(plain_times(logit_cotangent, head_weight), "section")
     top_cotangent = norm_backward(final, final_inverse, hidden_cotangent * final_gain).astype(
         jnp.bfloat16
     )

time: 483 us -> 507 us (1.050)
  waiting for transfers between devices: 399 us -> 417 us
  other arithmetic: 19 us -> 24.8 us
    all_gather x0 -> x1, waiting for transfers between devices: none -> 82.8 us  [_save_bars(): tmp = jnp.sum(lax.all_gather(mine, axis_name=a_name), axis=0)]
    psum x1 -> x0, waiting for transfers between devices: 64.8 us -> none  [local(): lax.psum(plain_times(logit_cotangent, head_weight), 'section')]
    reduce_sum x0 -> x1, other arithmetic: none -> 5.84 us  [_save_bars(): tmp = jnp.sum(lax.all_gather(mine, axis_name=a_name), axis=0)]
  transfers between devices with their start and end apart: 8 -> 8, of which waited for: 7 -> 7; matrix products, arithmetic and copies ran while one was open for 5% -> 6% of each run, Pallas kernels for 0% -> 0%
where the time goes in v1:
time: 507 us
  waiting for transfers between devices  417 us (82%)
  matrix products  26 us (5%)
  other arithmetic  24.8 us (5%)
  blocking collectives  15.2 us (3%)
  between operations  13.9 us (3%)
  local copies, waits for them, and re-layouts  5.23 us (1%)
    reduce_scatter x1, waiting for transfers between devices, local(): lax.psum_scatter(out_term, 'dp', scatter_dimension=0, tiled=True)  166 us
    all_gather x1, waiting for transfers between devices, _save_bars(): tmp = jnp.sum(lax.all_gather(mine, axis_name=a_name), axis=0)  82.8 us
    ppermute x3, waiting for transfers between devices, from_behind(): return lax.ppermute(block, axis, route)  74.8 us
    psum x1, waiting for transfers between devices, broadcast(): return lax.psum(kept, axis)  55.2 us
    reduce_scatter x1, waiting for transfers between devices, local(): lax.psum_scatter(embed_term(embed_master.shape[0] * lax.axis_size('dp')),...  37.8 us
    all_gather x2, blocking collectives, combined_all(): gathered = jax.tree.map(lambda a: lax.all_gather(a, axis), part)  15.2 us
    dot_general x3, matrix products, transposed_times(): lax.dot_general(former, latter, (((0,), (0,)), ((), ())), preferred_eleme...  14 us
    sub x3, other arithmetic, adam_update(): master - learning_rate * (first_next / (jnp.sqrt(second_next) + adam_eps)...  12.3 us
  transfers between devices with their start and end apart: 8, of which 7 were waited for; matrix products, arithmetic and copies ran while one was open for 6% of the time, Pallas kernels for 0%

profile of v1, /device:TPU:0, one launch (start us, length us, event | category | flops | bytes accessed | tf_op | source)
XLA Modules:
  0.0 506.6 jit_solution(6319605300927098642)
XLA Ops:
  7.3 7.8 %multiply_reduce_fusion.1 = (f32[256]{0:T(256)S(1)}, f32[256,2048]{1,0:T(8,128)}) fusion(bf16[256,2048]{1,0:T(8,128)(2,1)} %bitcast.44, bf16[1,2048,2048]{2,1,0:T(8,128)(2,1)} %param.25, bf16[256,2048]{1,0:T(8,128)(2,1)} %bitcast.54), kind=kOutput, calls=%fused_computation.15 | convolution fusion | flops 2149580544 | bytes 12583936 | tf_op jit(solution)/shard_map/dot_general | solution.py:42
  15.1 2.9 fusion.7
  18.1 55.2 %all-reduce.2.cloned.1.call-done = bf16[256,2048]{1,0:T(8,128)(2,1)} async-done(((bf16[256,2048]{1,0:T(8,128)(2,1)}), bf16[256,2048]{1,0:T(8,128)(2,1)}) %all-reduce.2.cloned.1.call-update) | async-done | bytes 1048592 | tf_op jit(solution)/shard_map/psum | solution.py:21
  73.3 2.0 fusion.23
  75.6 8.0 %all-gather.4 = f32[4,1,256]{2,1,0:T(1,128)S(1)} all-gather(f32[1,1,256]{2,1,0:T(1,128)S(1)} %bitcast.53), channel_id=3, replica_groups=mesh['section'=4,'dp'=8] {'section'}, dimensions={0}, use_global_device_ids=true | all-gather | bytes 5120 | tf_op jit(solution)/shard_map/all_gather | solution.py:25
  83.6 7.1 %all-gather.3 = f32[4,1,256]{2,1,0:T(1,128)S(1)} all-gather(f32[1,1,256]{2,1,0:T(1,128)S(1)} %bitcast.48), channel_id=2, replica_groups=mesh['section'=4,'dp'=8] {'section'}, dimensions={0}, use_global_device_ids=true | all-gather | bytes 5120 | tf_op jit(solution)/shard_map/all_gather | solution.py:25
  90.9 2.1 fusion.18
  93.1 1.1 copy-done.6
  94.3 2.9 fusion.16
  97.2 0.6 copy-done.15
  97.9 82.8 %all-gather.7.cloned.1.call-done = f32[1024,2048]{1,0:T(8,128)} async-done(((f32[256,2048]{1,0:T(8,128)}), f32[1024,2048]{1,0:T(8,128)}) %all-gather.7.cloned.1.call-update) | async-done | bytes 8388624 | tf_op jit(solution)/shard_map/all_gather | solution.py:15
  180.7 5.8 %reduce_sum.38 = f32[256,2048]{1,0:T(8,128)} reduce(f32[4,256,2048]{2,1,0:T(8,128)} %bitcast.43, f32[]{:T(128)} %constant.87.clone.1), dimensions={0}, to_apply=%region_6.7 | reduce | flops 1572864 | bytes 10485764 | tf_op jit(solution)/shard_map/reduce_sum | solution.py:15
  186.5 2.1 multiply_reduce_fusion
  188.8 0.9 copy-done.4
  189.7 0.5 multiply_convert_fusion
  190.2 79.6 %while.30 = (s32[]{:T(128)}, bf16[256,2048]{1,0:T(8,128)(2,1)S(1)}, pred[]{:T(512)}, s32[]{:T(128)}) while((s32[]{:T(128)}, bf16[256,2048]{1,0:T(8,128)(2,1)S(1)}, pred[]{:T(512)}, s32[]{:T(128)}) %tuple.77), condition=%wide.region_9.10_spmd, body=%wide.region_8.9_spmd.sunk | while | flops 524290 | bytes 7340126 | solution.py:146
  190.2 1.3 collective-permute-start
  191.5 25.0 %collective-permute-done = bf16[256,2048]{1,0:T(8,128)(2,1)S(1)} collective-permute-done((bf16[256,2048]{1,0:T(8,128)(2,1)S(1)}, bf16[256,2048]{1,0:T(8,128)(2,1)S(1)}, u32[]{:S(2)}, u32[]{:S(2)}) %collective-permute-start) | collective-permute-done | bytes 1048608 | tf_op jit(solution)/shard_map/while/body/eval_jaxpr/ppermute | solution.py:38
  216.8 1.3 collective-permute-start
  218.1 25.2 %collective-permute-done = bf16[256,2048]{1,0:T(8,128)(2,1)S(1)} collective-permute-done((bf16[256,2048]{1,0:T(8,128)(2,1)S(1)}, bf16[256,2048]{1,0:T(8,128)(2,1)S(1)}, u32[]{:S(2)}, u32[]{:S(2)}) %collective-permute-start) | collective-permute-done | bytes 1048608 | tf_op jit(solution)/shard_map/while/body/eval_jaxpr/ppermute | solution.py:38
  243.6 1.3 collective-permute-start
  244.9 24.6 %collective-permute-done = bf16[256,2048]{1,0:T(8,128)(2,1)S(1)} collective-permute-done((bf16[256,2048]{1,0:T(8,128)(2,1)S(1)}, bf16[256,2048]{1,0:T(8,128)(2,1)S(1)}, u32[]{:S(2)}, u32[]{:S(2)}) %collective-permute-start) | collective-permute-done | bytes 1048608 | tf_op jit(solution)/shard_map/while/body/eval_jaxpr/ppermute | solution.py:38
  269.5 0.3 broadcast_select_fusion.2
  269.7 2.8 fusion.11
  272.8 1.0 copy-done.5
  273.8 8.3 %fusion.24 = f32[2048,2048]{1,0:T(8,128)} fusion(bf16[256,2048]{1,0:T(8,128)(2,1)S(1)} %get-tuple-element.183, bf16[256,2048]{1,0:T(8,128)(2,1)S(1)} %bitcast.45), kind=kOutput, calls=%fused_computation.42 | convolution fusion | flops 2147483648 | bytes 18874368 | tf_op jit(solution)/shard_map/dot_general | solution.py:48
  282.2 0.9 copy-done.7
  283.5 2.4 multiply_subtract_fusion.2
  285.8 37.8 %reduce-scatter.8.cloned.1.call-done = f32[64,2048]{1,0:T(8,128)} async-done(((f32[512,2048]{1,0:T(8,128)}), f32[64,2048]{1,0:T(8,128)}) %reduce-scatter.8.cloned.1.call-update) | async-done | bytes 524304 | tf_op jit(solution)/shard_map/reduce_scatter | solution.py:156
  323.6 2.4 multiply_subtract_fusion.1
  326.0 166.5 %reduce-scatter.4.cloned.1.call-done = f32[256,2048]{1,0:T(8,128)} async-done(((f32[2048,2048]{1,0:T(8,128)}), f32[256,2048]{1,0:T(8,128)}) %reduce-scatter.4.cloned.1.call-update) | async-done | bytes 2097168 | tf_op jit(solution)/shard_map/reduce_scatter | solution.py:148
  492.5 7.6 %multiply_subtract_fusion = (f32[1,256,2048]{2,1,0:T(8,128)}, f32[1,256,2048]{2,1,0:T(8,128)}, f32[1,256,2048]{2,1,0:T(8,128)}) fusion(f32[1,256,2048]{2,1,0:T(8,128)} %param.27, f32[256,2048]{1,0:T(8,128)} %reduce-scatter.4.cloned.1.call-done, f32[1,256,2048]{2,1,0:T(8,128)} %param.29, f32[1,256,2048]{2,1,0:T(8,128)} %param.28), kind=kLoop, calls=%fused_computation.11 | loop fusion | flops 6815744 | bytes 14680064 | tf_op jit(solution)/shard_map/sub | solution.py:72
  (58 shorter events, 2.1 us)
Async XLA Ops:
  7.2 66.1 %copy-start = (bf16[512,2048]{1,0:T(8,128)(2,1)S(1)}, bf16[512,2048]{1,0:T(8,128)(2,1)}, u32[]{:S(2)}) copy-start(bf16[512,2048]{1,0:T(8,128)(2,1)} %param.26) | copy-start | bytes 6291460
  7.2 66.1 %all-reduce.2.cloned.1.call-start = ((), (), s32[]{:S(2)}) async-start(), calls=%async_computation.3 | async-start | bytes 2097152 | tf_op jit(solution)/shard_map/psum | solution.py:21
  7.2 7.8 %copy-start.13 = (f32[2048]{0:T(1024)S(1)}, f32[2048]{0:T(1024)}, u32[]{:S(2)}) copy-start(f32[2048]{0:T(1024)} %param.24) | copy-start | bytes 24580
  15.1 3.0 copy-start.14
  18.0 162.7 %all-gather.7.cloned.1.call-start = ((), (), s32[]{:S(2)}) async-start(), calls=%async_computation.7 | async-start | bytes 10485760 | tf_op jit(solution)/shard_map/all_gather | solution.py:15
  93.0 1.2 copy-start.6
  93.1 189.1 %reduce-scatter.6.cloned.1.call-start = ((), (), s32[]{:S(2)}) async-start(), calls=%async_computation.5 | async-start | bytes 4718592 | tf_op jit(solution)/shard_map/reduce_scatter | solution.py:135
  97.1 0.7 copy-start.15
  97.1 226.5 %reduce-scatter.8.cloned.1.call-start = ((), (), s32[]{:S(2)}) async-start(), calls=%async_computation.6 | async-start | bytes 4718592 | tf_op jit(solution)/shard_map/reduce_scatter | solution.py:156
  180.7 5.8 %copy-start.2 = (f32[256,2048]{1,0:T(8,128)S(1)}, f32[256,2048]{1,0:T(8,128)}, u32[]{:S(2)}) copy-start(f32[256,2048]{1,0:T(8,128)} %get-tuple-element.214) | copy-start | bytes 6291460
  186.5 2.2 copy-start.3
  186.5 3.2 copy-start.4
  190.2 26.3 %collective-permute-start = (bf16[256,2048]{1,0:T(8,128)(2,1)S(1)}, bf16[256,2048]{1,0:T(8,128)(2,1)S(1)}, u32[]{:S(2)}, u32[]{:S(2)}) collective-permute-start(bf16[256,2048]{1,0:T(8,128)(2,1)S(1)} %get-tuple-element.304), channel_id=1, source_target_pairs={{8,0},{16,8},{24,16},{9,1},{17,9},{25,17},{10,2},{18,10},{26,18},{... | collective-permute-start | bytes 3145736 | tf_op jit(solution)/shard_map/while/body/eval_jaxpr/ppermute | solution.py:38
  216.8 26.5 %collective-permute-start = (bf16[256,2048]{1,0:T(8,128)(2,1)S(1)}, bf16[256,2048]{1,0:T(8,128)(2,1)S(1)}, u32[]{:S(2)}, u32[]{:S(2)}) collective-permute-start(bf16[256,2048]{1,0:T(8,128)(2,1)S(1)} %get-tuple-element.304), channel_id=1, source_target_pairs={{8,0},{16,8},{24,16},{9,1},{17,9},{25,17},{10,2},{18,10},{26,18},{... | collective-permute-start | bytes 3145736 | tf_op jit(solution)/shard_map/while/body/eval_jaxpr/ppermute | solution.py:38
  243.6 25.9 %collective-permute-start = (bf16[256,2048]{1,0:T(8,128)(2,1)S(1)}, bf16[256,2048]{1,0:T(8,128)(2,1)S(1)}, u32[]{:S(2)}, u32[]{:S(2)}) collective-permute-start(bf16[256,2048]{1,0:T(8,128)(2,1)S(1)} %get-tuple-element.304), channel_id=1, source_target_pairs={{8,0},{16,8},{24,16},{9,1},{17,9},{25,17},{10,2},{18,10},{26,18},{... | collective-permute-start | bytes 3145736 | tf_op jit(solution)/shard_map/while/body/eval_jaxpr/ppermute | solution.py:38
  272.5 1.2 copy-start.5
  272.6 219.9 %reduce-scatter.4.cloned.1.call-start = ((), (), s32[]{:S(2)}) async-start(), calls=%async_computation.4 | async-start | bytes 18874368 | tf_op jit(solution)/shard_map/reduce_scatter | solution.py:148
  282.1 1.0 copy-start.7
  282.1 1.2 copy-start.8
  282.1 1.4 copy-start.9
  282.1 41.5 %copy-start.10 = (f32[64,2048]{1,0:T(8,128)S(1)}, f32[64,2048]{1,0:T(8,128)}, u32[]{:S(2)}) copy-start(f32[64,2048]{1,0:T(8,128)} %param.33) | copy-start | bytes 1572868
  282.1 41.5 %copy-start.11 = (f32[64,2048]{1,0:T(8,128)S(1)}, f32[64,2048]{1,0:T(8,128)}, u32[]{:S(2)}) copy-start(f32[64,2048]{1,0:T(8,128)} %param.35) | copy-start | bytes 1572868
  282.2 41.5 %copy-start.12 = (f32[64,2048]{1,0:T(8,128)S(1)}, f32[64,2048]{1,0:T(8,128)}, u32[]{:S(2)}) copy-start(f32[64,2048]{1,0:T(8,128)} %param.34) | copy-start | bytes 1572868
  492.5 7.6 %copy-start.1 = (bf16[512,2048]{1,0:T(8,128)(2,1)S(1)}, bf16[512,2048]{1,0:T(8,128)(2,1)}, u32[]{:S(2)}) copy-start(bf16[512,2048]{1,0:T(8,128)(2,1)} %param.26) | copy-start | bytes 6291460
Sparse Core Ops, SparseCore 0:
  18.1 55.1 all-reduce.1
  93.2 87.4 all-gather.6
  183.0 49.8 reduce-scatter.5
  272.7 50.8 reduce-scatter.7
  325.8 166.6 reduce-scatter.3
